TPU v7x, 32 devices: a whole 2x2x4 slice. The times are simulated.
32 devices in a mesh: graphs: 2 (over y), rows: 4 (over z), cols: 2 (over x), sub: 2 (over core).
Axes of the slice: x: 2, y: 2, z: 4, core: 2. Of those that a mesh axis runs over, the one named last changes fastest.
Arguments:
- current_block: float32 [16, 65536], P(None, ('graphs', 'rows', 'cols', 'sub')), parts along dimension 1, may hold values from -1200 to 1200, as said below
- previous_block: float32 [16, 65536], P(None, ('graphs', 'rows', 'cols', 'sub')), parts along dimension 1, may hold values from -1200 to 1200, as said below
- adjacency_tiles: float32 [1536, 128, 128], P(('graphs', 'rows', 'cols', 'sub')), parts along dimension 0, may hold values from -0.3125 to 0.3125
- tile_rows: int32 [1536], P(('graphs', 'rows', 'cols', 'sub')), parts along dimension 0, may hold values from 0 to 255, as said below
- tile_cols: int32 [1536], P(('graphs', 'rows', 'cols', 'sub')), parts along dimension 0, may hold values from 0 to 255, as said below
- tile_count: int32 [32], P(('graphs', 'rows', 'cols', 'sub')), parts along dimension 0, may hold values from 18 to 48, as said below
- locked: int32 [2], P('graphs'), parts along dimension 0, may hold values from 0 to 7
Outputs:
- w_basis: float32 [16, 65536], P(None, ('graphs', 'rows', 'cols', 'sub')), parts along dimension 1
- w_image: float32 [16, 65536], P(None, ('graphs', 'rows', 'cols', 'sub')), parts along dimension 1
- ritz_matrix: float32 [96, 48], P('graphs'), parts along dimension 0
There are 2 independent parts, one for each index of `graphs`. A program takes and returns all parts, laid end to end along the dimension named above; each array names one. Nothing has to cross between parts.
Inputs may be any that keep to these rules, and one draw needn't show every extreme that they name: `current_block`: entries of order one to some hundreds. `previous_block`: entries of order one to some hundreds. Slots d * 48 to (d + 1) * 48 - 1 belong to device d and name its own tile rows d * 16 to (d + 1) * 16 - 1. The first 16 slots of a device name its tile rows in order, with tile_cols equal to tile_rows. Slots past the device's count name tile row d * 16 and carry no weight. `tile_cols`: A slot of device d names a tile column from d * 16 - 8 to (d + 1) * 16 + 7. Slot 16 of a device names a tile of the block before it and slot 17 one of the block after it, where such a block exists. A pair of tile row and tile column may stand in several slots; their tiles add. `tile_count`: in every draw some device has all 48 slots live.
All inputs are finite; a program needn't handle non-finite values.
Results may differ from a plain program's by a relative error of at most 0.000094.
Values sent between devices are 32-bit elements; how exact they have to be, the bound alone decides.
A program may use at most 64 MiB of HBM per device.

v0:
```python
import jax
import jax.numpy as jnp
from jax import lax
from jax.sharding import PartitionSpec as P


def extended(cells, sides, width):
    for axis, dim in sides:
        count = lax.axis_size(axis)
        ends = count - 1
        head = lax.slice_in_dim(cells, 0, width, axis=dim)
        tail = lax.slice_in_dim(cells, cells.shape[dim] - width, cells.shape[dim], axis=dim)
        cells = jnp.concatenate(
            [
                lax.ppermute(tail, axis, [(i, (i + 1) % count) for i in range(ends)]),
                cells,
                lax.ppermute(head, axis, [((i + 1) % count, i) for i in range(ends)]),
            ],
            axis=dim,
        )
    return cells


def inner_products(left, right):
    return jnp.dot(left, right.T, precision=lax.Precision.HIGHEST)


def solve_lower(factor, values):
    return lax.linalg.triangular_solve(factor, values, left_side=True, lower=True)


def rayleigh_ritz(gram_b, gram_a):
    factor_b = jnp.linalg.cholesky(gram_b)
    symmetric = 0.5 * (gram_a + gram_a.T)
    halfway = solve_lower(factor_b, symmetric)
    return solve_lower(factor_b, halfway.T)


def operate(vectors, padded, adjacency_tiles, column_position, placing, span_tiles):
    channels, rows_here = vectors.shape
    tile_size = adjacency_tiles.shape[1]
    column_blocks = padded.reshape(channels, span_tiles, tile_size)
    gathered = jnp.take(column_blocks, column_position, axis=1)
    products = jnp.einsum(
        "cta,tab->ctb", gathered, adjacency_tiles, precision=lax.Precision.HIGHEST
    )
    summed = jnp.einsum("ctb,tr->crb", products, placing, precision=lax.Precision.HIGHEST)
    return vectors - summed.reshape(channels, rows_here)


def body(current_block, previous_block, adjacency_tiles, tile_rows, tile_cols, tile_count, locked):
    vectors_k, rows_here = current_block.shape
    tile_size = adjacency_tiles.shape[1]
    row_tiles = rows_here // tile_size
    slot_count = adjacency_tiles.shape[0]
    vertex_total = rows_here * lax.axis_size(("rows", "cols", "sub"))
    position = lax.axis_index(("rows", "cols", "sub"))
    reach_tiles = row_tiles // 2
    span_tiles = row_tiles + 2 * reach_tiles
    column_position = tile_cols - (position * row_tiles - reach_tiles)
    row_slot = tile_rows - position * row_tiles
    live_mask = (jnp.arange(slot_count, dtype=jnp.int32) < tile_count[0]).astype(jnp.float32)
    placing = (row_slot[:, None] == jnp.arange(row_tiles, dtype=jnp.int32)[None, :]).astype(
        jnp.float32
    )
    placing = placing * live_mask[:, None]
    stacked = jnp.concatenate([current_block, previous_block], axis=0)
    padded_pair = extended(stacked, ((("rows", "cols", "sub"), 1),), reach_tiles * tile_size)
    pair_image = operate(
        stacked, padded_pair, adjacency_tiles, column_position, placing, span_tiles
    )
    x_image = pair_image[:vectors_k]
    p_image = pair_image[vectors_k:]
    frozen_rows = jnp.arange(vectors_k, dtype=jnp.int32) < locked[0]
    frozen_diag = jnp.diag(frozen_rows.astype(jnp.float32))
    zero_rows = jnp.zeros((vectors_k,), jnp.float32)
    pad_diag = jnp.diag(jnp.concatenate([zero_rows, frozen_rows.astype(jnp.float32), zero_rows]))
    cross_sum, square_sum = lax.psum(
        (jnp.sum(current_block * x_image, axis=1), jnp.sum(current_block * current_block, axis=1)),
        ("rows", "cols", "sub"),
    )
    quotient = cross_sum / (square_sum + 1e-06)
    residual = jnp.where(frozen_rows[:, None], 0.0, x_image - quotient[:, None] * current_block)
    gram_w = (
        lax.psum(inner_products(residual, residual), ("rows", "cols", "sub")) / vertex_total
        + frozen_diag
    )
    factor = jnp.linalg.cholesky(gram_w)
    w_basis = solve_lower(factor, residual)
    padded = extended(w_basis, ((("rows", "cols", "sub"), 1),), reach_tiles * tile_size)
    w_image = operate(w_basis, padded, adjacency_tiles, column_position, placing, span_tiles)
    search = jnp.concatenate([current_block, w_basis, previous_block], axis=0)
    search_image = jnp.concatenate([x_image, w_image, p_image], axis=0)
    plain_sum, image_sum = lax.psum(
        (inner_products(search, search), inner_products(search, search_image)),
        ("rows", "cols", "sub"),
    )
    gram_b = plain_sum / vertex_total + pad_diag
    gram_a = image_sum / vertex_total
    ritz_matrix = rayleigh_ritz(gram_b, gram_a)
    return (w_basis, w_image, ritz_matrix)


def solution(mesh):
    in_specs = (
        P(None, ("graphs", "rows", "cols", "sub")),
        P(None, ("graphs", "rows", "cols", "sub")),
        P(("graphs", "rows", "cols", "sub"), None, None),
        P(("graphs", "rows", "cols", "sub")),
        P(("graphs", "rows", "cols", "sub")),
        P(("graphs", "rows", "cols", "sub")),
        P("graphs"),
    )
    out_specs = (
        P(None, ("graphs", "rows", "cols", "sub")),
        P(None, ("graphs", "rows", "cols", "sub")),
        P("graphs", None),
    )
    return jax.shard_map(body, mesh=mesh, in_specs=in_specs, out_specs=out_specs, check_vma=False)
```

profile of v0, /device:TPU:0, one launch (start us, length us, event | category | flops | bytes accessed | tf_op | source)
XLA Modules:
  0.0 182.3 jit_solution(9188400379763008146)
XLA Ops:
  0.6 0.0 copy-start
  0.6 1.1 constant_dynamic-update-slice_fusion.1
  1.7 0.9 constant_dynamic-update-slice_fusion
  2.6 0.7 fusion.54
  3.3 3.0 %collective-permute-start = (f32[32,1024]{1,0:T(8,128)}, f32[32,1024]{1,0:T(8,128)}, u32[]{:S(2)}, u32[]{:S(2)}) collective-permute-start(f32[32,1024]{1,0:T(8,128)} %get-tuple-element.14), channel_id=1, source_target_pairs={{0,1},{1,2},{2,3},{3,4},{4,5},{5,6},{6,7},{7,8},{8,9},{9,10},{10,1... | collective-permute-start | bytes 393224 | tf_op jit(solution)/shard_map/ppermute | solution.py:15
  6.4 1.3 collective-permute-start.1
  7.7 0.7 broadcast_subtract_fusion
  9.6 0.5 iota_compare_fusion.7
  10.1 0.0 copy-start.6
  10.1 0.7 compare_and_fusion
  10.8 0.6 pad_maximum_fusion.3
  11.4 0.0 copy-done.6
  11.4 0.0 collective-permute-done
  11.5 0.0 collective-permute-done.1
  11.5 1.8 %copy_bitcast_fusion = f32[32,32,128]{2,0,1:T(8,128)} fusion(f32[32,1024]{1,0:T(8,128)} %collective-permute-done.1, f32[32,2048]{1,0:T(8,128)S(1)} %constant_dynamic-update-slice_fusion, f32[32,1024]{1,0:T(8,128)} %collective-permute-done), kind=kLoop, calls=%fused_computation.9 | loop fusion | flops 262144 | bytes 1048576 | tf_op jit(solution)/shard_map/reshape | solution.py:42
  13.3 2.5 %gather_fusion = f32[48,32,128]{2,1,0:T(8,128)} fusion(f32[32,32,128]{2,0,1:T(8,128)} %copy_bitcast_fusion, s32[1024]{0:T(1024)S(1)} %pad_clamp_fusion), kind=kCustom, calls=%fused_computation | custom fusion | bytes 1573056 | tf_op jit(solution)/shard_map/jit(_take)/gather | solution.py:43
  15.8 0.0 copy-done
  15.8 0.0 copy-start.2
  15.8 4.0 %fusion.2 = f32[48,32,128]{2,1,0:T(8,128)S(1)} fusion(f32[48,128,128]{2,1,0:T(8,128)S(1)} %copy-done, f32[48,32,128]{2,1,0:T(8,128)} %gather_fusion, pred[48]{0:T(512)(128)(4,1)S(1)} %get-tuple-element.10), kind=kOutput, calls=%fused_computation.5 | convolution fusion | flops 302186496 | bytes 4718640 | tf_op jit(solution)/shard_map/cta,tab->ctb/dot_general | solution.py:44
  19.8 0.9 fusion
  20.7 0.1 bitcast_subtract_fusion
  20.8 0.0 copy-start.1
  20.8 0.7 copy-done.1
  21.5 0.0 copy-done.2
  21.5 0.8 multiply_reduce_fusion
  22.4 35.7 %all-reduce.1 = (f32[16]{0:T(128)S(1)}, f32[16]{0:T(128)S(1)}) all-reduce(f32[16]{0:T(128)S(1)} %get-tuple-element.5, f32[16]{0:T(128)S(1)} %get-tuple-element.4), channel_id=1, replica_groups=mesh['graphs'=2,'rows'=4,'cols'=2,'sub'=2] {'rows','cols','sub'}, use_global_device_ids=true, to_apply=%region_1.2 | all-reduce | flops 32 | bytes 256 | tf_op jit(solution)/shard_map/psum | solution.py:78
  58.1 1.3 fusion.53
  59.4 30.0 %psum.37 = f32[16,16]{1,0:T(8,128)S(1)} all-reduce(f32[16,16]{1,0:T(8,128)S(1)} %fusion.53), channel_id=1, replica_groups=mesh['graphs'=2,'rows'=4,'cols'=2,'sub'=2] {'rows','cols','sub'}, use_global_device_ids=true, to_apply=%region_4.5 | all-reduce | flops 256 | bytes 2048 | tf_op jit(solution)/shard_map/psum | solution.py:85
  89.5 0.7 select_add_fusion.1
  90.2 0.1 copy.17
  90.3 0.7 fusion.34
  91.0 1.4 cholesky.31
  92.5 0.6 compare_reduce_fusion.1
  93.1 0.6 fusion.31
  93.8 1.2 custom-call.12
  95.0 1.3 fusion.32
  96.3 0.0 copy-start.3
  96.3 1.8 collective-permute-start.2
  98.1 1.3 collective-permute-start.3
  99.4 2.0 %fusion.20 = f32[48,48]{0,1:T(8,128)} fusion(f32[16,2048]{1,0:T(8,128)} %param.10, f32[16,2048]{1,0:T(8,128)S(1)} %fusion.32, f32[16,2048]{1,0:T(8,128)S(1)} %copy-done.2), kind=kOutput, calls=%fused_computation.26 | convolution fusion | flops 56819712 | bytes 402432 | tf_op jit(solution)/shard_map/dot_general | solution.py:25
  101.5 0.0 collective-permute-done.2
  101.5 0.0 collective-permute-done.3
  101.5 0.7 copy_bitcast_fusion.1
  102.2 2.3 %gather_fusion.1 = f32[48,16,128]{2,1,0:T(8,128)} fusion(f32[16,32,128]{2,0,1:T(8,128)} %copy_bitcast_fusion.1, s32[1024]{0:T(1024)S(1)} %pad_clamp_fusion), kind=kCustom, calls=%fused_computation.1 | custom fusion | bytes 786624 | tf_op jit(solution)/shard_map/jit(_take)/gather | solution.py:43
  104.5 0.0 copy-start.5
  104.5 3.8 %fusion.14 = f32[48,16,128]{2,1,0:T(8,128)S(1)} fusion(f32[48,128,128]{2,1,0:T(8,128)S(1)} %copy-done, f32[48,16,128]{2,1,0:T(8,128)} %gather_fusion.1, pred[48]{0:T(512)(128)(4,1)S(1)} %get-tuple-element.10), kind=kOutput, calls=%fused_computation.20 | convolution fusion | flops 151093248 | bytes 3932208 | tf_op jit(solution)/shard_map/cta,tab->ctb/dot_general | solution.py:44
  108.3 0.4 fusion.12
  108.8 0.0 copy-start.4
  108.8 0.0 copy-done.3
  108.8 0.6 copy-done.4
  109.4 1.5 fusion.6
  110.9 60.5 %all-reduce = (f32[48,48]{0,1:T(8,128)S(1)}, f32[48,48]{0,1:T(8,128)S(1)}) all-reduce(f32[48,48]{0,1:T(8,128)S(1)} %fusion.6, f32[48,48]{0,1:T(8,128)} %fusion.20), channel_id=1, replica_groups=mesh['graphs'=2,'rows'=4,'cols'=2,'sub'=2] {'rows','cols','sub'}, use_global_device_ids=true, to_apply=%region_10.11 | all-reduce | flops 4608 | bytes 36864 | tf_op jit(solution)/shard_map/psum | solution.py:94
  171.4 0.1 copy.20
  171.5 0.0 copy-done.5
  171.5 0.1 select_add_fusion
  171.5 0.1 copy.21
  171.6 0.1 fusion.29
  171.7 4.4 %cholesky.65 = f32[48,48]{1,0:T(8,128)S(1)} custom-call(f32[48,48]{1,0:T(8,128)S(1)} %fusion.29), custom_call_target="Cholesky" | custom-call | tf_op jit(solution)/shard_map/jit(cholesky)/cholesky | solution.py:33
  176.1 0.6 compare_reduce_fusion
  176.8 0.7 fusion.23
  177.4 3.7 %custom-call.15 = f32[1,48,48]{1,2,0:T(8,128)S(1)} custom-call(f32[1,48,48]{2,1,0:T(8,128)S(1)} %fusion.23), custom_call_target="InvertDiagBlocksLowerTriangular" | custom-call | tf_op jit(solution)/shard_map/triangular_solve/custom-call.3 | solution.py:29
  181.1 0.1 copy.23
  181.2 0.2 convolution_bitcast_fusion
  181.4 0.8 fusion.27
  (10 shorter events, 0.1 us)
Async XLA Ops:
  0.6 15.2 %copy-start = (f32[48,128,128]{2,1,0:T(8,128)S(1)}, f32[48,128,128]{2,1,0:T(8,128)}, u32[]{:S(2)}) copy-start(f32[48,128,128]{2,1,0:T(8,128)} %param.11) | copy-start | bytes 9437188
  3.3 8.1 %collective-permute-start = (f32[32,1024]{1,0:T(8,128)}, f32[32,1024]{1,0:T(8,128)}, u32[]{:S(2)}, u32[]{:S(2)}) collective-permute-start(f32[32,1024]{1,0:T(8,128)} %get-tuple-element.14), channel_id=1, source_target_pairs={{0,1},{1,2},{2,3},{3,4},{4,5},{5,6},{6,7},{7,8},{8,9},{9,10},{10,1... | collective-permute-start | bytes 393224 | tf_op jit(solution)/shard_map/ppermute | solution.py:15
  6.4 5.1 %collective-permute-start.1 = (f32[32,1024]{1,0:T(8,128)S(1)}, f32[32,1024]{1,0:T(8,128)}, u32[]{:S(2)}, u32[]{:S(2)}) collective-permute-start(f32[32,1024]{1,0:T(8,128)S(1)} %get-tuple-element.15), channel_id=1, source_target_pairs={{1,0},{2,1},{3,2},{4,3},{5,4},{6,5},{7,6},{8,7},{9,8},{10,9},{11,1... | collective-permute-start | bytes 393224 | tf_op jit(solution)/shard_map/ppermute | solution.py:17
  10.1 1.3 copy-start.6
  15.8 5.7 %copy-start.2 = (f32[16,2048]{1,0:T(8,128)S(1)}, f32[16,2048]{1,0:T(8,128)}, u32[]{:S(2)}) copy-start(f32[16,2048]{1,0:T(8,128)} %param.9) | copy-start | bytes 393220
  20.8 0.7 copy-start.1
  96.3 12.5 %copy-start.3 = (f32[16,2048]{1,0:T(8,128)}, f32[16,2048]{1,0:T(8,128)S(1)}, u32[]{:S(2)}) copy-start(f32[16,2048]{1,0:T(8,128)S(1)} %fusion.32) | copy-start | bytes 393220
  96.3 5.2 %collective-permute-start.2 = (f32[16,1024]{1,0:T(8,128)S(1)}, f32[16,1024]{1,0:T(8,128)S(1)}, u32[]{:S(2)}, u32[]{:S(2)}) collective-permute-start(f32[16,1024]{1,0:T(8,128)S(1)} %get-tuple-element.16), channel_id=1, source_target_pairs={{0,1},{1,2},{2,3},{3,4},{4,5},{5,6},{6,7},{7,8},{8,9},{9,10},{10,1... | collective-permute-start | bytes 196616 | tf_op jit(solution)/shard_map/ppermute | solution.py:15
  98.1 3.4 %collective-permute-start.3 = (f32[16,1024]{1,0:T(8,128)S(1)}, f32[16,1024]{1,0:T(8,128)S(1)}, u32[]{:S(2)}, u32[]{:S(2)}) collective-permute-start(f32[16,1024]{1,0:T(8,128)S(1)} %get-tuple-element.17), channel_id=1, source_target_pairs={{1,0},{2,1},{3,2},{4,3},{5,4},{6,5},{7,6},{8,7},{9,8},{10,9},{11,1... | collective-permute-start | bytes 196616 | tf_op jit(solution)/shard_map/ppermute | solution.py:17
  104.5 67.0 %copy-start.5 = (f32[48]{0:T(128)S(1)}, f32[48]{0:T(128)}, u32[]{:S(2)}) copy-start(f32[48]{0:T(128)} %pad_maximum_fusion.3) | copy-start | bytes 580
  108.8 0.7 copy-start.4
where the time goes:
time: 183 us; the launch traced here: 182 us
  blocking collectives  126 us (69%)
  other arithmetic  21 us (11%)
  matrix products  16.3 us (9%)
  local copies, waits for them, and re-layouts  9.1 us (5%)
  starting transfers between devices  7.44 us (4%)
  between operations  2.15 us (1%)
    psum x1, blocking collectives, body(): lax.psum((inner_products(search, search), inner_products(search, search_i...  60.5 us
    psum x1, blocking collectives, body(): lax.psum((jnp.sum(current_block * x_image, axis=1), jnp.sum(current_block...  35.7 us
    psum x1, blocking collectives, body(): lax.psum(inner_products(residual, residual), ('rows', 'cols', 'sub'))  30 us
    dot_general x2, matrix products, operate(): jnp.einsum('cta,tab->ctb', gathered, adjacency_tiles, precision=lax.Preci...  7.77 us
    another operation x4, other arithmetic, solve_lower(): lax.linalg.triangular_solve(factor, values, left_side=True, lower=True)  6.2 us
    another operation x3, other arithmetic, rayleigh_ritz(): factor_b = jnp.linalg.cholesky(gram_b)  5.06 us
    ppermute x2, starting transfers between devices, extended(): lax.ppermute(tail, axis, [(i, (i + 1) % count) for i in range(ends)])  4.87 us
    dot_general x3, matrix products, inner_products(): return jnp.dot(left, right.T, precision=lax.Precision.HIGHEST)  4.86 us
  transfers between devices with their start and end apart: 4, of which 0 were waited for; matrix products, arithmetic and copies ran while one was open for 2% of the time, Pallas kernels for 0%

commit v1 on v0

v1 whole, which is shorter than its diff:
```python
import functools

import jax
import jax.numpy as jnp
from jax import lax
from jax.experimental import pallas as pl
from jax.experimental.pallas import tpu as pltpu
from jax.sharding import PartitionSpec as P

MESH = pl.DeviceIdType.MESH
F32 = jnp.float32
BF16 = jnp.bfloat16
HIGHEST = lax.Precision.HIGHEST
NT_DIMS = (((1,), (1,)), ((), ()))


def split(values):
    high = values.astype(BF16)
    return high, (values - high.astype(F32)).astype(BF16)


def iota(shape, dim):
    return lax.broadcasted_iota(jnp.int32, shape, dim)


def gather_kernel(
    sizes,
    cols_ref, rows_ref, count_ref, locked_ref, x_ref, p_ref, tiles_ref,
    r_ref, ar_ref, gram_ref,
    raw, halves, xh, ph, yh, q_buf, z_buf, extra, mine_q, near_q, line_q, far_q, mine_g, near_g, line_g, far_g,
    tile_sem, halo_send, halo_recv, near_send, near_recv, far_send, far_recv,
):
    row_count, col_count, sub_count = sizes
    near_count = col_count * sub_count
    vectors, here = x_ref.shape
    slots, tile, _ = tiles_ref.shape
    row_tiles = here // tile
    reach = row_tiles // 2
    spare = slots - row_tiles
    chunk = row_tiles // 2
    chunks = slots // chunk

    row_at = lax.axis_index("rows")
    near_at = lax.axis_index("cols") * sub_count + lax.axis_index("sub")
    position = row_at * near_count + near_at
    total = row_count * near_count

    def place(spot):
        return {
            "rows": spot // near_count,
            "cols": (spot % near_count) // sub_count,
            "sub": spot % sub_count,
        }

    def near_device(index):
        return {"cols": index // sub_count, "sub": index % sub_count}

    def far_device(index):
        return {"rows": index}

    tile_copies = []
    for c in range(chunks):
        part = pl.ds(c * chunk, chunk)
        tile_copies.append(pltpu.make_async_copy(tiles_ref.at[part], raw.at[part], tile_sem.at[c]))
        tile_copies[-1].start()

    has_left = position > 0
    has_right = position < total - 1
    barrier = pltpu.get_barrier_semaphore()

    @pl.when(has_left)
    def _():
        pl.semaphore_signal(barrier, inc=1, device_id=place(position - 1), device_id_type=MESH)

    @pl.when(has_right)
    def _():
        pl.semaphore_signal(barrier, inc=1, device_id=place(position + 1), device_id_type=MESH)

    for k in range(1, near_count):
        pl.semaphore_signal(
            barrier, inc=1, device_id=near_device((near_at + k) % near_count), device_id_type=MESH
        )
    for k in range(1, row_count):
        pl.semaphore_signal(
            barrier, inc=1, device_id=far_device((row_at + k) % row_count), device_id_type=MESH
        )
    for t in range(row_tiles):
        xh[reach + t] = x_ref[:, t * tile : (t + 1) * tile]
        ph[reach + t] = p_ref[:, t * tile : (t + 1) * tile]
    expected = near_count + row_count - 2
    pl.semaphore_wait(
        barrier, expected + has_left.astype(jnp.int32) + has_right.astype(jnp.int32)
    )

    def halo_copies(buffer, which):
        left = pltpu.make_async_remote_copy(
            src_ref=buffer.at[pl.ds(reach, reach)],
            dst_ref=buffer.at[pl.ds(reach + row_tiles, reach)],
            send_sem=halo_send.at[which, 0],
            recv_sem=halo_recv.at[which, 0],
            device_id=place(position - 1),
            device_id_type=MESH,
        )
        right = pltpu.make_async_remote_copy(
            src_ref=buffer.at[pl.ds(row_tiles, reach)],
            dst_ref=buffer.at[pl.ds(0, reach)],
            send_sem=halo_send.at[which, 1],
            recv_sem=halo_recv.at[which, 1],
            device_id=place(position + 1),
            device_id_type=MESH,
        )
        return left, right

    def halo_start(copies):
        left, right = copies

        @pl.when(has_left)
        def _():
            left.start()

        @pl.when(has_right)
        def _():
            right.start()

    def halo_arrived(copies):
        left, right = copies

        @pl.when(has_right)
        def _():
            left.wait_recv()

        @pl.when(has_left)
        def _():
            right.wait_recv()

    def halo_sent(copies):
        left, right = copies

        @pl.when(has_left)
        def _():
            left.wait_send()

        @pl.when(has_right)
        def _():
            right.wait_send()

    x_halo = halo_copies(xh, 0)
    p_halo = halo_copies(ph, 1)
    y_halo = halo_copies(yh, 2)
    halo_start(x_halo)
    halo_start(p_halo)

    def product(block, slot):
        high, low = split(block)
        lhs = jnp.concatenate(
            [jnp.concatenate([high, high], axis=1), jnp.concatenate([low, low], axis=1)], axis=0
        )
        out = jnp.dot(lhs, halves[slot], preferred_element_type=F32)
        return out[:vectors] + out[vectors:]

    def flat(buffer, start):
        return jnp.concatenate([buffer[start + t] for t in range(row_tiles)], axis=1)

    def split_tiles(c):
        tile_copies[c].wait()

        def step(i, carry):
            t = c * chunk + i
            high, low = split(raw[t])
            halves[t, 0:tile, :] = high
            halves[t, tile : 2 * tile, :] = low
            return carry

        lax.fori_loop(0, chunk, step, 0)

    def diagonal(source, target, target_base):
        def step(g, carry):
            for i in range(8):
                r = g * 8 + i
                target[target_base + r] = product(source[reach + r], r)
            return carry

        lax.fori_loop(0, row_tiles // 8, step, 0)

    live = count_ref[0]
    base_col = position * row_tiles - reach
    base_row = position * row_tiles
    places = [
        jnp.where(row_tiles + t < live, rows_ref[row_tiles + t] - base_row, -1) for t in range(spare)
    ]

    def scattered(padded, target, target_base):
        def step(g, carry):
            for i in range(8):
                t = g * 8 + i
                index = jnp.clip(cols_ref[row_tiles + t] - base_col, 0, 2 * row_tiles - 1)
                extra[t] = product(padded[index], row_tiles + t)
            return carry

        lax.fori_loop(0, spare // 8, step, 0)

        def gather(r, carry):
            sums = [target[target_base + r], None, None, None]
            for t in range(spare):
                term = extra[t] * jnp.where(places[t] == r, 1.0, 0.0).astype(F32)
                sums[t % 4] = term if sums[t % 4] is None else sums[t % 4] + term
            target[target_base + r] = (sums[0] + sums[1]) + (sums[2] + sums[3])
            return carry

        lax.fori_loop(0, row_tiles, gather, 0)

    def exchange(mine, buffer, count, at, device, send, recv, which):
        copies = []
        for k in range(1, count):
            other = (at + k) % count
            copies.append(
                (
                    pltpu.make_async_remote_copy(
                        src_ref=mine,
                        dst_ref=buffer.at[at],
                        send_sem=send.at[which, k],
                        recv_sem=recv.at[which, at],
                        device_id=device(other),
                        device_id_type=MESH,
                    ),
                    pltpu.make_async_remote_copy(
                        src_ref=mine,
                        dst_ref=buffer.at[other],
                        send_sem=send.at[which, k],
                        recv_sem=recv.at[which, other],
                        device_id=device(other),
                        device_id_type=MESH,
                    ),
                )
            )
        for out, _ in copies:
            out.start()
        buffer[at] = mine[...]
        return copies

    def collect(copies, buffer, count):
        for _, arriving in copies:
            arriving.wait_recv()
        out = buffer[0]
        for k in range(1, count):
            out = out + buffer[k]
        return out

    def flush(copies):
        for out, _ in copies:
            out.wait_send()

    for c in range(chunks):
        split_tiles(c)
        if c == row_tiles // chunk - 1:
            diagonal(xh, yh, reach)
    diagonal(ph, q_buf, 0)
    halo_arrived(x_halo)
    scattered(xh, yh, reach)
    halo_start(y_halo)

    x = x_ref[...]
    xx = jnp.sum(x * x, axis=1, keepdims=True)
    y = flat(yh, reach)
    xy = jnp.sum(x * y, axis=1, keepdims=True)
    lane = iota((vectors, 128), 1)
    line = iota((vectors, 128), 0)
    on_first = lane == line
    on_second = lane == line + vectors
    mine_q[...] = jnp.sum(
        jnp.where(on_first, xx, 0.0) + jnp.where(on_second, xy, 0.0), axis=0, keepdims=True
    )
    near_copies = exchange(mine_q, near_q, near_count, near_at, near_device, near_send, near_recv, 0)

    halo_arrived(p_halo)
    scattered(ph, q_buf, 0)

    line_q[...] = collect(near_copies, near_q, near_count)
    far_copies = exchange(line_q, far_q, row_count, row_at, far_device, far_send, far_recv, 0)
    diagonal(yh, z_buf, 0)
    halo_arrived(y_halo)
    scattered(yh, z_buf, 0)

    sums = jnp.broadcast_to(collect(far_copies, far_q, row_count), (vectors, 128))
    xx_all = jnp.sum(jnp.where(on_first, sums, 0.0), axis=1, keepdims=True)
    xy_all = jnp.sum(jnp.where(on_second, sums, 0.0), axis=1, keepdims=True)
    shift = (xy_all + 1e-06) / (xx_all + 1e-06)
    free = iota((vectors, 1), 0) >= locked_ref[0]
    y = flat(yh, reach)
    z = flat(z_buf, 0)
    p = p_ref[...]
    residual = jnp.where(free, shift * x - y, 0.0)
    residual_image = residual - jnp.where(free, shift * y - z, 0.0)
    r_ref[...] = residual
    ar_ref[...] = residual_image
    search = [split(v) for v in (x, residual, p)]
    image = [split(v) for v in (x - y, residual_image, p - flat(q_buf, 0))]
    left = jnp.concatenate([v[0] for v in search] + [v[1] for v in search], axis=0)
    right_high = jnp.concatenate([v[0] for v in search] + [v[0] for v in image], axis=0)
    right_low = jnp.concatenate([v[1] for v in search] + [v[1] for v in image], axis=0)
    full = lax.dot_general(left, right_high, NT_DIMS, preferred_element_type=F32)
    full = full + lax.dot_general(left, right_low, NT_DIMS, preferred_element_type=F32)
    width = 3 * vectors
    mine_g[...] = jnp.zeros_like(mine_g)
    mine_g[:, 0 : 2 * width] = full[:width] + full[width:]
    near_g_copies = exchange(
        mine_g, near_g, near_count, near_at, near_device, near_send, near_recv, 1
    )
    line_g[...] = collect(near_g_copies, near_g, near_count)
    far_g_copies = exchange(line_g, far_g, row_count, row_at, far_device, far_send, far_recv, 1)
    gram_ref[...] = collect(far_g_copies, far_g, row_count)

    halo_sent(x_halo)
    halo_sent(p_halo)
    halo_sent(y_halo)
    flush(near_copies)
    flush(far_copies)
    flush(near_g_copies)
    flush(far_g_copies)


def finish_kernel(vertex_total, locked_ref, r_ref, ar_ref, gram_ref, w_ref, aw_ref, ritz_ref, upper):
    vectors = r_ref.shape[0]
    width = 3 * vectors
    scale = 1.0 / vertex_total
    gram = gram_ref[...] * scale
    locked = locked_ref[0]

    lane = iota((width, 128), 1)
    line = iota((width, 128), 0)
    padded = (line == lane) & (line >= vectors) & (line < vectors + locked)
    big = jnp.where(lane < width, gram + jnp.where(padded, 1.0, 0.0), 0.0)
    big = big + jnp.where(lane == line + width, 1.0, 0.0)

    lane_w = iota((vectors, 128), 1)
    line_w = iota((vectors, 128), 0)
    frozen = (lane_w == line_w + vectors) & (line_w < locked)
    small = gram[vectors : 2 * vectors] + jnp.where(frozen, 1.0, 0.0)
    small = jnp.where((lane_w >= vectors) & (lane_w < 2 * vectors), small, 0.0)
    small = small + jnp.where(lane_w == line_w + 2 * vectors, 1.0, 0.0)

    def eliminate(matrix, k, pivot_lane):
        row = matrix[k : k + 1, :]
        pivot = row[:, pivot_lane : pivot_lane + 1]
        column = matrix[:, pivot_lane : pivot_lane + 1]
        return matrix - column * (row / pivot), row * lax.rsqrt(pivot)

    small_rows = []
    for k in range(vectors):
        small, row = eliminate(small, k, vectors + k)
        small_rows.append(row)
    inverse_w = jnp.concatenate(small_rows, axis=0)[:, 2 * vectors : 3 * vectors]
    w_ref[...] = jnp.dot(inverse_w, r_ref[...], precision=HIGHEST, preferred_element_type=F32)
    aw_ref[...] = jnp.dot(inverse_w, ar_ref[...], precision=HIGHEST, preferred_element_type=F32)

    for k in range(width):
        big, row = eliminate(big, k, k)
        upper[k : k + 1, :] = row
    inverse = upper[:, width : 2 * width]
    image = gram[:, width : 2 * width]
    half = jnp.dot(inverse, image, precision=HIGHEST, preferred_element_type=F32)
    first = lax.dot_general(half, inverse, NT_DIMS, precision=HIGHEST, preferred_element_type=F32)
    second = lax.dot_general(inverse, half, NT_DIMS, precision=HIGHEST, preferred_element_type=F32)
    ritz_ref[...] = 0.5 * (first + second)


def body(sizes, current_block, previous_block, adjacency_tiles, tile_rows, tile_cols, tile_count, locked):
    vectors, here = current_block.shape
    slots, tile, _ = adjacency_tiles.shape
    row_tiles = here // tile
    row_count, col_count, sub_count = sizes
    near_count = col_count * sub_count
    chunks = slots // (row_tiles // 2)
    width = 3 * vectors
    smem = pl.BlockSpec(memory_space=pltpu.SMEM)
    vmem = pl.BlockSpec(memory_space=pltpu.VMEM)
    anywhere = pl.BlockSpec(memory_space=pl.ANY)
    dma = pltpu.SemaphoreType.DMA
    residual, residual_image, gram = pl.pallas_call(
        functools.partial(gather_kernel, sizes),
        out_shape=(
            jax.ShapeDtypeStruct((vectors, here), F32),
            jax.ShapeDtypeStruct((vectors, here), F32),
            jax.ShapeDtypeStruct((width, 128), F32),
        ),
        in_specs=[smem] * 4 + [vmem] * 2 + [anywhere],
        out_specs=(vmem, vmem, vmem),
        scratch_shapes=[
            pltpu.VMEM((slots, tile, tile), F32),
            pltpu.VMEM((slots, 2 * tile, tile), BF16),
            pltpu.VMEM((2 * row_tiles, vectors, tile), F32),
            pltpu.VMEM((2 * row_tiles, vectors, tile), F32),
            pltpu.VMEM((2 * row_tiles, vectors, tile), F32),
            pltpu.VMEM((row_tiles, vectors, tile), F32),
            pltpu.VMEM((row_tiles, vectors, tile), F32),
            pltpu.VMEM((slots - row_tiles, vectors, tile), F32),
            pltpu.VMEM((1, 128), F32),
            pltpu.VMEM((near_count, 1, 128), F32),
            pltpu.VMEM((1, 128), F32),
            pltpu.VMEM((row_count, 1, 128), F32),
            pltpu.VMEM((width, 128), F32),
            pltpu.VMEM((near_count, width, 128), F32),
            pltpu.VMEM((width, 128), F32),
            pltpu.VMEM((row_count, width, 128), F32),
            dma((chunks,)),
            dma((3, 2)),
            dma((3, 2)),
            dma((2, near_count)),
            dma((2, near_count)),
            dma((2, row_count)),
            dma((2, row_count)),
        ],
        compiler_params=pltpu.CompilerParams(collective_id=0, has_side_effects=True),
        name="operator_and_grams",
    )(tile_cols, tile_rows, tile_count, locked, current_block, previous_block, adjacency_tiles)
    vertex_total = here * row_count * near_count
    return pl.pallas_call(
        functools.partial(finish_kernel, vertex_total),
        out_shape=(
            jax.ShapeDtypeStruct((vectors, here), F32),
            jax.ShapeDtypeStruct((vectors, here), F32),
            jax.ShapeDtypeStruct((width, width), F32),
        ),
        in_specs=[smem] + [vmem] * 3,
        out_specs=(vmem, vmem, vmem),
        scratch_shapes=[pltpu.VMEM((width, 128), F32)],
        name="factor_and_project",
    )(locked, residual, residual_image, gram)


def solution(mesh):
    split_all = ("graphs", "rows", "cols", "sub")
    sizes = tuple(mesh.shape[name] for name in ("rows", "cols", "sub"))
    in_specs = (
        P(None, split_all),
        P(None, split_all),
        P(split_all, None, None),
        P(split_all),
        P(split_all),
        P(split_all),
        P("graphs"),
    )
    out_specs = (P(None, split_all), P(None, split_all), P("graphs", None))
    return jax.shard_map(
        functools.partial(body, sizes), mesh=mesh, in_specs=in_specs, out_specs=out_specs, check_vma=False
    )
```

time: 183 us -> 34.4 us (0.19)
  blocking collectives: 126 us -> 0 us
  Pallas kernels: 0 us -> 32.3 us
  other arithmetic: 21 us -> 0 us
  matrix products: 16.3 us -> 0 us
  local copies, waits for them, and re-layouts: 9.1 us -> 0 us
  starting transfers between devices: 7.44 us -> 0 us
    psum x3 -> x0, blocking collectives: 126 us -> none  [the longest x1 60.5 us: body(): lax.psum((inner_products(search, search), inner_products(search, search_i...]
    pallas_call x0 -> x2, Pallas kernels: none -> 32.3 us  [the longest x1 26.2 us: body(): pl.pallas_call(functools.partial(gather_kernel, sizes), out_shape=(jax.Sh...]
    dot_general x7 -> x0, matrix products: 14 us -> none  [the longest x2 7.77 us: operate(): jnp.einsum('cta,tab->ctb', gathered, adjacency_tiles, precision=lax.Preci...]
    another operation x10 -> x0, other arithmetic: 13.4 us -> none  [the longest x4 6.2 us: solve_lower(): lax.linalg.triangular_solve(factor, values, left_side=True, lower=True)]
    ppermute x4 -> x0, starting transfers between devices: 7.44 us -> none  [the longest x2 4.87 us: extended(): lax.ppermute(tail, axis, [(i, (i + 1) % count) for i in range(ends)])]
    gather x2 -> x0, local copies, waits for them, and re-layouts: 4.78 us -> none  [operate(): gathered = jnp.take(column_blocks, column_position, axis=1)]
    reshape x2 -> x0, other arithmetic: 2.55 us -> none  [operate(): column_blocks = padded.reshape(channels, span_tiles, tile_size)]
    unnamed x15 -> x0, local copies, waits for them, and re-layouts: 2.42 us -> none
  transfers between devices with their start and end apart: 4 -> 0, of which waited for: 0 -> 0; matrix products, arithmetic and copies ran while one was open for 2% -> 0% of each run, Pallas kernels for 0% -> 0%
where the time goes in v1:
time: 34.4 us; the launch traced here: 34.2 us
  Pallas kernels  32.3 us (94%)
  between operations  1.93 us (6%)
    pallas_call x1, Pallas kernels, body(): pl.pallas_call(functools.partial(gather_kernel, sizes), out_shape=(jax.Sh...  26.2 us
    pallas_call x1, Pallas kernels, body(): pl.pallas_call(functools.partial(finish_kernel, vertex_total), out_shape=...  6.09 us

profile of v1, /device:TPU:0, one launch (start us, length us, event | category | flops | bytes accessed | tf_op | source)
XLA Modules:
  0.0 34.2 jit_solution(1232124546219020088)
XLA Ops:
  1.9 26.2 %operator_and_grams.1 = (f32[16,2048]{1,0:T(8,128)}, f32[16,2048]{1,0:T(8,128)}, f32[48,128]{1,0:T(8,128)}) custom-call(s32[48]{0:T(128)} %cols_ref.1, s32[48]{0:T(128)} %rows_ref.1, s32[1]{0:T(128)S(6)} %copy.10.count_ref, s32[1]{0:T(128)S(6)} %copy.11.locked_ref, f32[16,2048]{1,0:T(8,128)} %x_ref.1, f32[16,2048]{1,0:T(8,128)} %p_ref.1, ...), custom_call_target="tpu_custom_call" | custom-call | tf_op jit(solution)/shard_map/operator_and_grams/pallas_call | solution.py:379
  28.1 6.1 %factor_and_project.1 = (f32[16,2048]{1,0:T(8,128)}, f32[16,2048]{1,0:T(8,128)}, f32[48,48]{1,0:T(8,128)}) custom-call(s32[1]{0:T(128)S(6)} %copy.11.locked_ref, f32[16,2048]{1,0:T(8,128)} %get-tuple-element.6.r_ref, f32[16,2048]{1,0:T(8,128)} %get-tuple-element.7.ar_ref, f32[48,128]{1,0:T(8,128)} %get-tuple-element.8.gram_ref), custom_call_target="tpu_custom_call" | custom-call | tf_op jit(solution)/shard_map/factor_and_project/pallas_call | solution.py:417

commit v2 on v1

--- a/solution.py
+++ b/solution.py
@@ -25,10 +25,10 @@
 
 def gather_kernel(
     sizes,
-    cols_ref, rows_ref, count_ref, locked_ref, x_ref, p_ref, tiles_ref,
-    r_ref, ar_ref, gram_ref,
-    raw, halves, xh, ph, yh, q_buf, z_buf, extra, mine_q, near_q, line_q, far_q, mine_g, near_g, line_g, far_g,
-    tile_sem, halo_send, halo_recv, near_send, near_recv, far_send, far_recv,
+    cols_ref, rows_ref, count_ref, locked_ref, x_hbm, p_hbm, tiles_ref,
+    r_ref, ar_ref, early_ref, late_ref,
+    x_ref, p_ref, raw, halves, xh, ph, yh, q_buf, z_buf, extra, mine_q, near_q, line_q, far_q,
+    mine_e, near_e, line_e, far_e, mine_g, near_g, line_g, far_g, block_sem, tile_sem, halo_send, halo_recv, near_send, near_recv, far_send, far_recv,
 ):
     row_count, col_count, sub_count = sizes
     near_count = col_count * sub_count
@@ -58,6 +58,12 @@
     def far_device(index):
         return {"rows": index}
 
+    block_copies = (
+        pltpu.make_async_copy(x_hbm, x_ref, block_sem.at[0]),
+        pltpu.make_async_copy(p_hbm, p_ref, block_sem.at[1]),
+    )
+    for copy in block_copies:
+        copy.start()
     tile_copies = []
     for c in range(chunks):
         part = pl.ds(c * chunk, chunk)
@@ -84,6 +90,8 @@
         pl.semaphore_signal(
             barrier, inc=1, device_id=far_device((row_at + k) % row_count), device_id_type=MESH
         )
+    for copy in block_copies:
+        copy.wait()
     for t in range(row_tiles):
         xh[reach + t] = x_ref[:, t * tile : (t + 1) * tile]
         ph[reach + t] = p_ref[:, t * tile : (t + 1) * tile]
@@ -190,24 +198,22 @@
     ]
 
     def scattered(padded, target, target_base):
-        def step(g, carry):
-            for i in range(8):
-                t = g * 8 + i
-                index = jnp.clip(cols_ref[row_tiles + t] - base_col, 0, 2 * row_tiles - 1)
-                extra[t] = product(padded[index], row_tiles + t)
+        for t in range(spare):
+            index = jnp.clip(cols_ref[row_tiles + t] - base_col, 0, 2 * row_tiles - 1)
+            extra[t] = product(padded[index], row_tiles + t)
+
+        def gather(g, carry):
+            some = [g * 4 + i for i in range(4)]
+            sums = [target[target_base + r] for r in some]
+            for t in range(spare):
+                block = extra[t]
+                for i, r in enumerate(some):
+                    sums[i] = sums[i] + block * jnp.where(places[t] == r, 1.0, 0.0).astype(F32)
+            for i, r in enumerate(some):
+                target[target_base + r] = sums[i]
             return carry
 
-        lax.fori_loop(0, spare // 8, step, 0)
-
-        def gather(r, carry):
-            sums = [target[target_base + r], None, None, None]
-            for t in range(spare):
-                term = extra[t] * jnp.where(places[t] == r, 1.0, 0.0).astype(F32)
-                sums[t % 4] = term if sums[t % 4] is None else sums[t % 4] + term
-            target[target_base + r] = (sums[0] + sums[1]) + (sums[2] + sums[3])
-            return carry
-
-        lax.fori_loop(0, row_tiles, gather, 0)
+        lax.fori_loop(0, row_tiles // 4, gather, 0)
 
     def exchange(mine, buffer, count, at, device, send, recv, which):
         copies = []
@@ -274,10 +280,34 @@
 
     halo_arrived(p_halo)
     scattered(ph, q_buf, 0)
+    p = p_ref[...]
+    x_parts, y_parts, p_parts, q_parts = [split(v) for v in (x, y, p, flat(q_buf, 0))]
+    gap = jnp.zeros((vectors, here), BF16)
+
+    def inner(left, right):
+        lhs = jnp.concatenate([v[0] for v in left] + [v[1] for v in left], axis=0)
+        out = None
+        for half in range(2):
+            rhs = jnp.concatenate([gap if v is None else v[half] for v in right], axis=0)
+            term = lax.dot_general(lhs, rhs, NT_DIMS, preferred_element_type=F32)
+            out = term if out is None else out + term
+        count = len(left) * vectors
+        return out[:count] + out[count:]
+
+    wide = 6 * vectors
+    mine_e[...] = jnp.zeros_like(mine_e)
+    mine_e[:, 0:wide] = inner(
+        (x_parts, p_parts), (x_parts, None, p_parts, y_parts, None, q_parts)
+    )
+    near_e_copies = exchange(
+        mine_e, near_e, near_count, near_at, near_device, near_send, near_recv, 1
+    )
 
     line_q[...] = collect(near_copies, near_q, near_count)
     far_copies = exchange(line_q, far_q, row_count, row_at, far_device, far_send, far_recv, 0)
     diagonal(yh, z_buf, 0)
+    line_e[...] = collect(near_e_copies, near_e, near_count)
+    far_e_copies = exchange(line_e, far_e, row_count, row_at, far_device, far_send, far_recv, 1)
     halo_arrived(y_halo)
     scattered(yh, z_buf, 0)
 
@@ -286,82 +316,134 @@
     xy_all = jnp.sum(jnp.where(on_second, sums, 0.0), axis=1, keepdims=True)
     shift = (xy_all + 1e-06) / (xx_all + 1e-06)
     free = iota((vectors, 1), 0) >= locked_ref[0]
-    y = flat(yh, reach)
-    z = flat(z_buf, 0)
-    p = p_ref[...]
     residual = jnp.where(free, shift * x - y, 0.0)
-    residual_image = residual - jnp.where(free, shift * y - z, 0.0)
+    carried = jnp.where(free, shift * y - flat(z_buf, 0), 0.0)
     r_ref[...] = residual
-    ar_ref[...] = residual_image
-    search = [split(v) for v in (x, residual, p)]
-    image = [split(v) for v in (x - y, residual_image, p - flat(q_buf, 0))]
-    left = jnp.concatenate([v[0] for v in search] + [v[1] for v in search], axis=0)
-    right_high = jnp.concatenate([v[0] for v in search] + [v[0] for v in image], axis=0)
-    right_low = jnp.concatenate([v[1] for v in search] + [v[1] for v in image], axis=0)
-    full = lax.dot_general(left, right_high, NT_DIMS, preferred_element_type=F32)
-    full = full + lax.dot_general(left, right_low, NT_DIMS, preferred_element_type=F32)
-    width = 3 * vectors
+    ar_ref[...] = residual - carried
+    r_parts, n_parts = split(residual), split(carried)
+    plain = inner((r_parts,), (x_parts, r_parts, p_parts, y_parts, n_parts, q_parts))
+    other = inner((n_parts,), (x_parts, r_parts, p_parts, x_parts, r_parts, p_parts))
+    first_half = iota((vectors, wide), 1) < 3 * vectors
     mine_g[...] = jnp.zeros_like(mine_g)
-    mine_g[:, 0 : 2 * width] = full[:width] + full[width:]
+    mine_g[:, 0:wide] = jnp.where(first_half, plain, 0.5 * (plain + other))
     near_g_copies = exchange(
-        mine_g, near_g, near_count, near_at, near_device, near_send, near_recv, 1
+        mine_g, near_g, near_count, near_at, near_device, near_send, near_recv, 2
     )
     line_g[...] = collect(near_g_copies, near_g, near_count)
-    far_g_copies = exchange(line_g, far_g, row_count, row_at, far_device, far_send, far_recv, 1)
-    gram_ref[...] = collect(far_g_copies, far_g, row_count)
+    far_g_copies = exchange(line_g, far_g, row_count, row_at, far_device, far_send, far_recv, 2)
+    early_ref[...] = collect(far_e_copies, far_e, row_count)
+    late_ref[...] = collect(far_g_copies, far_g, row_count)
 
     halo_sent(x_halo)
     halo_sent(p_halo)
     halo_sent(y_halo)
     flush(near_copies)
     flush(far_copies)
+    flush(near_e_copies)
+    flush(far_e_copies)
     flush(near_g_copies)
     flush(far_g_copies)
 
 
-def finish_kernel(vertex_total, locked_ref, r_ref, ar_ref, gram_ref, w_ref, aw_ref, ritz_ref, upper):
-    vectors = r_ref.shape[0]
+def finish_kernel(
+    vertex_total, locked_ref, r_hbm, ar_hbm, early_ref, late_ref, w_hbm, aw_hbm, ritz_ref,
+    upper, r_buf, ar_buf, w_buf, aw_buf, in_sem, out_sem,
+):
+    vectors = r_buf.shape[0]
     width = 3 * vectors
+    ins = (
+        pltpu.make_async_copy(r_hbm, r_buf, in_sem.at[0]),
+        pltpu.make_async_copy(ar_hbm, ar_buf, in_sem.at[1]),
+    )
+    outs = (
+        pltpu.make_async_copy(w_buf, w_hbm, out_sem.at[0]),
+        pltpu.make_async_copy(aw_buf, aw_hbm, out_sem.at[1]),
+    )
+    for copy in ins:
+        copy.start()
     scale = 1.0 / vertex_total
-    gram = gram_ref[...] * scale
+    early = early_ref[...] * scale
+    late = late_ref[...] * scale
     locked = locked_ref[0]
+
+    lane_w = iota((vectors, 128), 1)
+    line_w = iota((vectors, 128), 0)
+    frozen = (lane_w == line_w + vectors) & (line_w < locked)
+    small = late + jnp.where(frozen, 1.0, 0.0)
+    small = jnp.where((lane_w >= vectors) & (lane_w < 2 * vectors), small, 0.0)
+    small = small + jnp.where(lane_w == line_w + 2 * vectors, 1.0, 0.0)
 
     lane = iota((width, 128), 1)
     line = iota((width, 128), 0)
+    outer = (line < vectors) | (line >= 2 * vectors)
+    pick = jnp.concatenate(
+        [
+            jnp.where(outer & (lane == line), 1.0, 0.0),
+            jnp.where(outer & (lane == line + width), 1.0, 0.0),
+        ],
+        axis=1,
+    )
+    above = jnp.zeros((vectors, 128), F32)
+    set_first = jnp.concatenate([above, late, above, above, above, above, above, above], axis=0)
+    set_second = jnp.concatenate([above, above, above, above, late, above, above, above], axis=0)
+    turned = lax.dot_general(
+        pick, jnp.concatenate([set_first, set_second], axis=1), NT_DIMS,
+        precision=HIGHEST, preferred_element_type=F32,
+    )
+    gram = jnp.concatenate([early[:vectors], late, early[vectors:]], axis=0) + turned
     padded = (line == lane) & (line >= vectors) & (line < vectors + locked)
     big = jnp.where(lane < width, gram + jnp.where(padded, 1.0, 0.0), 0.0)
     big = big + jnp.where(lane == line + width, 1.0, 0.0)
 
-    lane_w = iota((vectors, 128), 1)
-    line_w = iota((vectors, 128), 0)
-    frozen = (lane_w == line_w + vectors) & (line_w < locked)
-    small = gram[vectors : 2 * vectors] + jnp.where(frozen, 1.0, 0.0)
-    small = jnp.where((lane_w >= vectors) & (lane_w < 2 * vectors), small, 0.0)
-    small = small + jnp.where(lane_w == line_w + 2 * vectors, 1.0, 0.0)
-
-    def eliminate(matrix, k, pivot_lane):
-        row = matrix[k : k + 1, :]
-        pivot = row[:, pivot_lane : pivot_lane + 1]
-        column = matrix[:, pivot_lane : pivot_lane + 1]
-        return matrix - column * (row / pivot), row * lax.rsqrt(pivot)
-
+    def panel(matrix, k, shift, count):
+        rows = [matrix[k + i : k + i + 1, :] for i in range(count)]
+        columns = [
+            jnp.broadcast_to(matrix[:, shift + k + i : shift + k + i + 1], matrix.shape)
+            for i in range(count)
+        ]
+        block = {
+            (i, j): jnp.broadcast_to(rows[i][:, shift + k + j : shift + k + j + 1], (1, 128))
+            for i in range(count)
+            for j in range(i, count)
+        }
+        done = []
+        for m in range(count):
+            inverse = 1.0 / block[m, m]
+            done.append(rows[m] * lax.rsqrt(block[m, m]))
+            factors = {j: block[m, j] * inverse for j in range(m + 1, count)}
+            for i in range(m + 1, count):
+                for j in range(i, count):
+                    block[i, j] = block[i, j] - factors[i] * block[m, j]
+                rows[i] = rows[i] - factors[i] * rows[m]
+                columns[i] = columns[i] - factors[i] * columns[m]
+            matrix = matrix - columns[m] * (rows[m] * inverse)
+        return matrix, done
+
+    step = 4
     small_rows = []
-    for k in range(vectors):
-        small, row = eliminate(small, k, vectors + k)
-        small_rows.append(row)
+    for k in range(0, vectors, step):
+        small, done = panel(small, k, vectors, step)
+        small_rows += done
     inverse_w = jnp.concatenate(small_rows, axis=0)[:, 2 * vectors : 3 * vectors]
-    w_ref[...] = jnp.dot(inverse_w, r_ref[...], precision=HIGHEST, preferred_element_type=F32)
-    aw_ref[...] = jnp.dot(inverse_w, ar_ref[...], precision=HIGHEST, preferred_element_type=F32)
-
-    for k in range(width):
-        big, row = eliminate(big, k, k)
-        upper[k : k + 1, :] = row
+    for copy in ins:
+        copy.wait()
+    w_buf[...] = jnp.dot(inverse_w, r_buf[...], precision=HIGHEST, preferred_element_type=F32)
+    outs[0].start()
+    aw_buf[...] = jnp.dot(inverse_w, ar_buf[...], precision=HIGHEST, preferred_element_type=F32)
+    outs[1].start()
+
+    for k in range(0, width, step):
+        big, done = panel(big, k, 0, step)
+        for i in range(step):
+            upper[k + i : k + i + 1, :] = done[i]
     inverse = upper[:, width : 2 * width]
-    image = gram[:, width : 2 * width]
+    image = gram[:, :width] - gram[:, width : 2 * width]
     half = jnp.dot(inverse, image, precision=HIGHEST, preferred_element_type=F32)
     first = lax.dot_general(half, inverse, NT_DIMS, precision=HIGHEST, preferred_element_type=F32)
     second = lax.dot_general(inverse, half, NT_DIMS, precision=HIGHEST, preferred_element_type=F32)
     ritz_ref[...] = 0.5 * (first + second)
+    for copy in outs:
+        copy.wait()
 
 
 def body(sizes, current_block, previous_block, adjacency_tiles, tile_rows, tile_cols, tile_count, locked):
@@ -376,16 +458,19 @@
     vmem = pl.BlockSpec(memory_space=pltpu.VMEM)
     anywhere = pl.BlockSpec(memory_space=pl.ANY)
     dma = pltpu.SemaphoreType.DMA
-    residual, residual_image, gram = pl.pallas_call(
+    residual, residual_image, early, late = pl.pallas_call(
         functools.partial(gather_kernel, sizes),
         out_shape=(
             jax.ShapeDtypeStruct((vectors, here), F32),
             jax.ShapeDtypeStruct((vectors, here), F32),
-            jax.ShapeDtypeStruct((width, 128), F32),
+            jax.ShapeDtypeStruct((2 * vectors, 128), F32),
+            jax.ShapeDtypeStruct((vectors, 128), F32),
         ),
-        in_specs=[smem] * 4 + [vmem] * 2 + [anywhere],
-        out_specs=(vmem, vmem, vmem),
+        in_specs=[smem] * 4 + [anywhere] * 3,
+        out_specs=(vmem, vmem, vmem, vmem),
         scratch_shapes=[
+            pltpu.VMEM((vectors, here), F32),
+            pltpu.VMEM((vectors, here), F32),
             pltpu.VMEM((slots, tile, tile), F32),
             pltpu.VMEM((slots, 2 * tile, tile), BF16),
             pltpu.VMEM((2 * row_tiles, vectors, tile), F32),
@@ -398,17 +483,22 @@
             pltpu.VMEM((near_count, 1, 128), F32),
             pltpu.VMEM((1, 128), F32),
             pltpu.VMEM((row_count, 1, 128), F32),
-            pltpu.VMEM((width, 128), F32),
-            pltpu.VMEM((near_count, width, 128), F32),
-            pltpu.VMEM((width, 128), F32),
-            pltpu.VMEM((row_count, width, 128), F32),
+            pltpu.VMEM((2 * vectors, 128), F32),
+            pltpu.VMEM((near_count, 2 * vectors, 128), F32),
+            pltpu.VMEM((2 * vectors, 128), F32),
+            pltpu.VMEM((row_count, 2 * vectors, 128), F32),
+            pltpu.VMEM((vectors, 128), F32),
+            pltpu.VMEM((near_count, vectors, 128), F32),
+            pltpu.VMEM((vectors, 128), F32),
+            pltpu.VMEM((row_count, vectors, 128), F32),
+            dma((2,)),
             dma((chunks,)),
             dma((3, 2)),
             dma((3, 2)),
-            dma((2, near_count)),
-            dma((2, near_count)),
-            dma((2, row_count)),
-            dma((2, row_count)),
+            dma((3, near_count)),
+            dma((3, near_count)),
+            dma((3, row_count)),
+            dma((3, row_count)),
         ],
         compiler_params=pltpu.CompilerParams(collective_id=0, has_side_effects=True),
         name="operator_and_grams",
@@ -421,11 +511,13 @@
             jax.ShapeDtypeStruct((vectors, here), F32),
             jax.ShapeDtypeStruct((width, width), F32),
         ),
-        in_specs=[smem] + [vmem] * 3,
-        out_specs=(vmem, vmem, vmem),
-        scratch_shapes=[pltpu.VMEM((width, 128), F32)],
+        in_specs=[smem] + [anywhere] * 2 + [vmem] * 2,
+        out_specs=(anywhere, anywhere, vmem),
+        scratch_shapes=[pltpu.VMEM((width, 128), F32)]
+        + [pltpu.VMEM((vectors, here), F32)] * 4
+        + [dma((2,)), dma((2,))],
         name="factor_and_project",
-    )(locked, residual, residual_image, gram)
+    )(locked, residual, residual_image, early, late)
 
 
 def solution(mesh):

time: 34.4 us -> 32.7 us (0.951)
  Pallas kernels: 32.3 us -> 30.4 us
    pallas_call x1, Pallas kernels: 6.09 us -> 4.62 us  [body(): pl.pallas_call(functools.partial(finish_kernel, vertex_total), out_shape=...]
    pallas_call x1, Pallas kernels: 26.2 us -> 25.8 us  [body(): pl.pallas_call(functools.partial(gather_kernel, sizes), out_shape=(jax.Sh...]
where the time goes in v2:
time: 32.7 us; the launch traced here: 32.3 us
  Pallas kernels  30.4 us (93%)
  between operations  1.93 us (6%)
    pallas_call x1, Pallas kernels, body(): pl.pallas_call(functools.partial(gather_kernel, sizes), out_shape=(jax.Sh...  25.8 us
    pallas_call x1, Pallas kernels, body(): pl.pallas_call(functools.partial(finish_kernel, vertex_total), out_shape=...  4.62 us

profile of v2, /device:TPU:0, one launch (start us, length us, event | category | flops | bytes accessed | tf_op | source)
XLA Modules:
  0.0 32.3 jit_solution(11239194849662573739)
XLA Ops:
  1.9 25.8 %operator_and_grams.1 = (f32[16,2048]{1,0:T(8,128)}, f32[16,2048]{1,0:T(8,128)}, f32[32,128]{1,0:T(8,128)}, f32[16,128]{1,0:T(8,128)}) custom-call(s32[48]{0:T(128)} %cols_ref.1, s32[48]{0:T(128)} %rows_ref.1, s32[1]{0:T(128)S(6)} %copy.10.count_ref, s32[1]{0:T(128)S(6)} %copy.11.locked_ref, f32[16,2048]{1,0:T(8,128)} %x_hbm.1, f32[16,2048]{1,0:T(8,128)} %p_hbm.1, ...), custom_call_target="tpu_custom_call" | custom-call | tf_op jit(solution)/shard_map/operator_and_grams/pallas_call | solution.py:461
  27.7 4.6 %factor_and_project.1 = (f32[16,2048]{1,0:T(8,128)}, f32[16,2048]{1,0:T(8,128)}, f32[48,48]{1,0:T(8,128)}) custom-call(s32[1]{0:T(128)S(6)} %copy.11.locked_ref, f32[16,2048]{1,0:T(8,128)} %get-tuple-element.7.r_hbm, f32[16,2048]{1,0:T(8,128)} %get-tuple-element.8.ar_hbm, f32[32,128]{1,0:T(8,128)} %get-tuple-element.9.early_ref, ...), custom_call_target="tpu_custom_call" | custom-call | tf_op jit(solution)/shard_map/factor_and_project/pallas_call | solution.py:507

commit v3 on v2

--- a/solution.py
+++ b/solution.py
@@ -26,9 +26,9 @@
 def gather_kernel(
     sizes,
     cols_ref, rows_ref, count_ref, locked_ref, x_hbm, p_hbm, tiles_ref,
-    r_ref, ar_ref, early_ref, late_ref,
-    x_ref, p_ref, raw, halves, xh, ph, yh, q_buf, z_buf, extra, mine_q, near_q, line_q, far_q,
-    mine_e, near_e, line_e, far_e, mine_g, near_g, line_g, far_g, block_sem, tile_sem, halo_send, halo_recv, near_send, near_recv, far_send, far_recv,
+    r_hbm, ar_hbm, early_ref, late_ref,
+    x_ref, p_ref, r_ref, ar_ref, raw, halves, xh, ph, yh, q_buf, z_buf, extra, mine_q, near_q, line_q, far_q,
+    mine_e, near_e, line_e, far_e, mine_g, near_g, line_g, far_g, block_sem, out_sem, tile_sem, halo_send, halo_recv, near_send, near_recv, far_send, far_recv,
 ):
     row_count, col_count, sub_count = sizes
     near_count = col_count * sub_count
@@ -306,8 +306,6 @@
     line_q[...] = collect(near_copies, near_q, near_count)
     far_copies = exchange(line_q, far_q, row_count, row_at, far_device, far_send, far_recv, 0)
     diagonal(yh, z_buf, 0)
-    line_e[...] = collect(near_e_copies, near_e, near_count)
-    far_e_copies = exchange(line_e, far_e, row_count, row_at, far_device, far_send, far_recv, 1)
     halo_arrived(y_halo)
     scattered(yh, z_buf, 0)
 
@@ -320,6 +318,12 @@
     carried = jnp.where(free, shift * y - flat(z_buf, 0), 0.0)
     r_ref[...] = residual
     ar_ref[...] = residual - carried
+    outs = (
+        pltpu.make_async_copy(r_ref, r_hbm, out_sem.at[0]),
+        pltpu.make_async_copy(ar_ref, ar_hbm, out_sem.at[1]),
+    )
+    for copy in outs:
+        copy.start()
     r_parts, n_parts = split(residual), split(carried)
     plain = inner((r_parts,), (x_parts, r_parts, p_parts, y_parts, n_parts, q_parts))
     other = inner((n_parts,), (x_parts, r_parts, p_parts, x_parts, r_parts, p_parts))
@@ -329,11 +333,15 @@
     near_g_copies = exchange(
         mine_g, near_g, near_count, near_at, near_device, near_send, near_recv, 2
     )
+    line_e[...] = collect(near_e_copies, near_e, near_count)
+    far_e_copies = exchange(line_e, far_e, row_count, row_at, far_device, far_send, far_recv, 1)
     line_g[...] = collect(near_g_copies, near_g, near_count)
     far_g_copies = exchange(line_g, far_g, row_count, row_at, far_device, far_send, far_recv, 2)
     early_ref[...] = collect(far_e_copies, far_e, row_count)
     late_ref[...] = collect(far_g_copies, far_g, row_count)
 
+    for copy in outs:
+        copy.wait()
     halo_sent(x_halo)
     halo_sent(p_halo)
     halo_sent(y_halo)
@@ -419,20 +427,24 @@
             matrix = matrix - columns[m] * (rows[m] * inverse)
         return matrix, done
 
+    for copy in ins:
+        copy.wait()
     step = 4
     small_rows = []
     for k in range(0, vectors, step):
         small, done = panel(small, k, vectors, step)
         small_rows += done
     inverse_w = jnp.concatenate(small_rows, axis=0)[:, 2 * vectors : 3 * vectors]
-    for copy in ins:
-        copy.wait()
-    w_buf[...] = jnp.dot(inverse_w, r_buf[...], precision=HIGHEST, preferred_element_type=F32)
-    outs[0].start()
-    aw_buf[...] = jnp.dot(inverse_w, ar_buf[...], precision=HIGHEST, preferred_element_type=F32)
-    outs[1].start()
-
     for k in range(0, width, step):
+        if k == 2 * vectors:
+            w_buf[...] = jnp.dot(
+                inverse_w, r_buf[...], precision=HIGHEST, preferred_element_type=F32
+            )
+            aw_buf[...] = jnp.dot(
+                inverse_w, ar_buf[...], precision=HIGHEST, preferred_element_type=F32
+            )
+            for copy in outs:
+                copy.start()
         big, done = panel(big, k, 0, step)
         for i in range(step):
             upper[k + i : k + i + 1, :] = done[i]
@@ -467,8 +479,10 @@
             jax.ShapeDtypeStruct((vectors, 128), F32),
         ),
         in_specs=[smem] * 4 + [anywhere] * 3,
-        out_specs=(vmem, vmem, vmem, vmem),
+        out_specs=(anywhere, anywhere, vmem, vmem),
         scratch_shapes=[
+            pltpu.VMEM((vectors, here), F32),
+            pltpu.VMEM((vectors, here), F32),
             pltpu.VMEM((vectors, here), F32),
             pltpu.VMEM((vectors, here), F32),
             pltpu.VMEM((slots, tile, tile), F32),
@@ -491,6 +505,7 @@
             pltpu.VMEM((near_count, vectors, 128), F32),
             pltpu.VMEM((vectors, 128), F32),
             pltpu.VMEM((row_count, vectors, 128), F32),
+            dma((2,)),
             dma((2,)),
             dma((chunks,)),
             dma((3, 2)),

time: 32.7 us -> 32.6 us (level)
  no operation moved by 1% of the time
where the time goes in v3:
time: 32.6 us; the launch traced here: 32.2 us
  Pallas kernels  30.3 us (93%)
  between operations  1.93 us (6%)
    pallas_call x1, Pallas kernels, body(): pl.pallas_call(functools.partial(gather_kernel, sizes), out_shape=(jax.Sh...  25.7 us
    pallas_call x1, Pallas kernels, body(): pl.pallas_call(functools.partial(finish_kernel, vertex_total), out_shape=...  4.62 us

profile of v3, /device:TPU:0, one launch (start us, length us, event | category | flops | bytes accessed | tf_op | source)
XLA Modules:
  0.0 32.2 jit_solution(10004066267525576657)
XLA Ops:
  1.9 25.7 %operator_and_grams.1 = (f32[16,2048]{1,0:T(8,128)}, f32[16,2048]{1,0:T(8,128)}, f32[32,128]{1,0:T(8,128)}, f32[16,128]{1,0:T(8,128)}) custom-call(s32[48]{0:T(128)} %cols_ref.1, s32[48]{0:T(128)} %rows_ref.1, s32[1]{0:T(128)S(6)} %copy.10.count_ref, s32[1]{0:T(128)S(6)} %copy.11.locked_ref, f32[16,2048]{1,0:T(8,128)} %x_hbm.1, f32[16,2048]{1,0:T(8,128)} %p_hbm.1, ...), custom_call_target="tpu_custom_call" | custom-call | tf_op jit(solution)/shard_map/operator_and_grams/pallas_call | solution.py:473
  27.6 4.6 %factor_and_project.1 = (f32[16,2048]{1,0:T(8,128)}, f32[16,2048]{1,0:T(8,128)}, f32[48,48]{1,0:T(8,128)}) custom-call(s32[1]{0:T(128)S(6)} %copy.11.locked_ref, f32[16,2048]{1,0:T(8,128)} %get-tuple-element.7.r_hbm, f32[16,2048]{1,0:T(8,128)} %get-tuple-element.8.ar_hbm, f32[32,128]{1,0:T(8,128)} %get-tuple-element.9.early_ref, ...), custom_call_target="tpu_custom_call" | custom-call | tf_op jit(solution)/shard_map/factor_and_project/pallas_call | solution.py:522
